TPU v7x, 32 devices: a whole 2x2x4 slice. The times are simulated.
32 devices in a mesh: row: 8 (over y, x, core), col: 4 (over z).
Axes of the slice: x: 2, y: 2, z: 4, core: 2. Of those that a mesh axis runs over, the one named last changes fastest.
Arguments:
- trailing: bfloat16 [4096, 8192], P('row', 'col'), may hold values from -6 to 6
- col_u: bfloat16 [8, 512, 64], P('row', 'col'), may hold values from -6 to 6
- col_v: bfloat16 [8, 512, 64], P('row', 'col'), may hold values from -0.75 to 0.75
- row_u: bfloat16 [16, 512, 64], P('col', 'row'), may hold values from -6 to 6
- row_v: bfloat16 [16, 512, 64], P('col', 'row'), may hold values from -0.03125 to 0.03125
- diag_lower_inv: float32 [512, 512], replicated, may hold values from -0.176776695 to 1, as said below
- diag_upper_inv: float32 [512, 512], replicated, may hold values from -0.176776695 to 2, as said below
Outputs:
- schur: bfloat16 [4096, 8192], P('row', 'col')
Inputs may be any that keep to these rules, and one draw needn't show every extreme that they name: `diag_lower_inv`: lower triangular with unit diagonal. `diag_upper_inv`: upper triangular with diagonal entries between 0.5 and 2.
All inputs are finite; a program needn't handle non-finite values.
Results may differ from a plain program's by a relative error of at most 0.0054.
Values may be sent and summed in bfloat16 or wider, within the bound.
A program may use at most 64 MiB of HBM per device.

v0:
```python
import jax
import jax.numpy as jnp
from jax import lax
from jax.sharding import PartitionSpec as P


def shards(trailing, col_u, col_v, row_u, row_v, diag_lower_inv, diag_upper_inv):
    highest = lax.Precision.HIGHEST
    whole_col_u, whole_col_v = (
        lax.all_gather(col_u, "col", axis=1, tiled=True),
        lax.all_gather(col_v, "col", axis=1, tiled=True),
    )
    left_v = jnp.einsum(
        "ba,tbr->tar", diag_upper_inv, whole_col_v.astype(jnp.float32), precision=highest
    )
    lower = jnp.einsum(
        "tpr,tar->tpa", whole_col_u.astype(jnp.float32), left_v, precision=highest
    ).astype(jnp.bfloat16)
    whole_row_u, whole_row_v = (
        lax.all_gather(row_u, "row", axis=1, tiled=True),
        lax.all_gather(row_v, "row", axis=1, tiled=True),
    )
    right_u = jnp.einsum(
        "ab,tbr->tar", diag_lower_inv, whole_row_u.astype(jnp.float32), precision=highest
    )
    upper_flip = jnp.einsum(
        "tar,tqr->tqa", right_u, whole_row_v.astype(jnp.float32), precision=highest
    ).astype(jnp.bfloat16)
    order = lower.shape[2]
    lower_flat = lower.reshape(-1, order)
    upper_flat = upper_flip.reshape(-1, order)
    product = lax.dot_general(
        lower_flat, upper_flat, (((1,), (1,)), ((), ())), preferred_element_type=jnp.float32
    )
    return (trailing.astype(jnp.float32) - product).astype(jnp.bfloat16)


def solution(mesh):
    placed = (
        P("row", "col"),
        P("row", "col", None),
        P("row", "col", None),
        P("col", "row", None),
        P("col", "row", None),
        P(),
        P(),
    )
    return jax.shard_map(
        shards, mesh=mesh, in_specs=placed, out_specs=P("row", "col"), check_vma=False
    )
```

profile of v0, /device:TPU:1, one launch (start us, length us, event | category | flops | bytes accessed | tf_op | source)
XLA Modules:
  0.0 53.8 jit_solution(7023791033043279824)
XLA Ops:
  0.0 0.0 copy-start
  0.0 0.0 copy-start.1
  0.0 10.9 %all_gather.13 = bf16[1,512,64]{1,2,0:T(8,128)(2,1)S(1)} all-gather(bf16[1,128,64]{1,2,0:T(8,128)(2,1)} %param.8), channel_id=1, replica_groups=mesh['row'=8,'col'=4] {'col'}, dimensions={1}, use_global_device_ids=true | all-gather | bytes 81920 | tf_op jit(solution)/shard_map/all_gather | solution.py:10
  10.9 9.6 %all_gather.12 = bf16[1,512,64]{1,2,0:T(8,128)(2,1)S(1)} all-gather(bf16[1,128,64]{1,2,0:T(8,128)(2,1)} %param.9), channel_id=1, replica_groups=mesh['row'=8,'col'=4] {'col'}, dimensions={1}, use_global_device_ids=true | all-gather | bytes 81920 | tf_op jit(solution)/shard_map/all_gather | solution.py:11
  20.5 0.0 copy-start.2
  20.5 1.8 %fusion.3 = f32[64,512]{1,0:T(8,128)S(1)} fusion(f32[512,512]{1,0:T(8,128)} %param.13, bf16[1,512,64]{1,2,0:T(8,128)(2,1)S(1)} %all_gather.12), kind=kOutput, calls=%fused_computation.6 | convolution fusion | flops 201326592 | bytes 1245184 | tf_op jit(solution)/shard_map/ba,tbr->tar/dot_general | solution.py:13
  22.3 0.6 %convolution_convert_fusion.1 = bf16[512,512]{1,0:T(8,128)(2,1)S(1)} fusion(f32[64,512]{1,0:T(8,128)S(1)} %fusion.3, bf16[1,512,64]{1,2,0:T(8,128)(2,1)S(1)} %all_gather.13), kind=kOutput, calls=%fused_computation.2 | convolution fusion | flops 201588736 | bytes 720896 | tf_op jit(solution)/shard_map/tpr,tar->tpa/dot_general | solution.py:16
  22.9 0.0 copy-done.1
  22.9 15.4 %all_gather.14 = bf16[4,512,64]{2,1,0:T(8,128)(2,1)S(1)} all-gather(bf16[4,64,64]{2,1,0:T(8,128)(2,1)S(1)} %copy-done.1), channel_id=1, replica_groups=mesh['row'=8,'col'=4] {'row'}, dimensions={1}, use_global_device_ids=true | all-gather | bytes 294912 | tf_op jit(solution)/shard_map/all_gather | solution.py:20
  38.4 0.0 copy-done
  38.4 1.0 %fusion = f32[4,64,512]{2,1,0:T(8,128)S(1)} fusion(bf16[4,512,64]{2,1,0:T(8,128)(2,1)S(1)} %all_gather.14, f32[512,512]{1,0:T(8,128)S(1)} %copy-done), kind=kOutput, calls=%fused_computation.3 | convolution fusion | flops 805306368 | bytes 1835008 | tf_op jit(solution)/shard_map/ab,tbr->tar/dot_general | solution.py:23
  39.4 0.0 copy-done.2
  39.4 0.0 copy-start.3
  39.4 10.0 %all_gather.15 = bf16[4,512,64]{2,1,0:T(8,128)(2,1)S(1)} all-gather(bf16[4,64,64]{2,1,0:T(8,128)(2,1)S(1)} %copy-done.2), channel_id=1, replica_groups=mesh['row'=8,'col'=4] {'row'}, dimensions={1}, use_global_device_ids=true | all-gather | bytes 294912 | tf_op jit(solution)/shard_map/all_gather | solution.py:21
  49.4 1.8 %convolution_convert_fusion = bf16[4,512,512]{1,2,0:T(8,128)(2,1)S(1)} fusion(f32[4,64,512]{2,1,0:T(8,128)S(1)} %fusion, bf16[4,512,64]{2,1,0:T(8,128)(2,1)S(1)} %all_gather.15), kind=kOutput, calls=%fused_computation.1 | convolution fusion | flops 806354944 | bytes 2883584 | tf_op jit(solution)/shard_map/tar,tqr->tqa/dot_general | solution.py:26
  51.2 0.0 copy-done.3
  51.2 2.6 %subtract_convert_fusion = bf16[512,2048]{1,0:T(8,128)(2,1)} fusion(bf16[512,2048]{1,0:T(8,128)(2,1)S(1)} %copy-done.3, bf16[512,512]{1,0:T(8,128)(2,1)S(1)} %convolution_convert_fusion.1, bf16[2048,512]{1,0:T(8,128)(2,1)S(1)} %bitcast.19), kind=kOutput, calls=%fused_computation | convolution fusion | flops 1076887552 | bytes 6815744 | tf_op jit(solution)/shard_map/dot_general | solution.py:32
Async XLA Ops:
  0.0 38.4 %copy-start = (f32[512,512]{1,0:T(8,128)S(1)}, f32[512,512]{1,0:T(8,128)}, u32[]{:S(2)}) copy-start(f32[512,512]{1,0:T(8,128)} %param.12) | copy-start | bytes 3145732
  0.0 22.9 %copy-start.1 = (bf16[4,64,64]{2,1,0:T(8,128)(2,1)S(1)}, bf16[4,64,64]{2,1,0:T(8,128)(2,1)}, u32[]{:S(2)}) copy-start(bf16[4,64,64]{2,1,0:T(8,128)(2,1)} %param.10) | copy-start | bytes 98308
  20.5 18.9 %copy-start.2 = (bf16[4,64,64]{2,1,0:T(8,128)(2,1)S(1)}, bf16[4,64,64]{2,1,0:T(8,128)(2,1)}, u32[]{:S(2)}) copy-start(bf16[4,64,64]{2,1,0:T(8,128)(2,1)} %param.11) | copy-start | bytes 98308
  39.4 11.8 %copy-start.3 = (bf16[512,2048]{1,0:T(8,128)(2,1)S(1)}, bf16[512,2048]{1,0:T(8,128)(2,1)}, u32[]{:S(2)}) copy-start(bf16[512,2048]{1,0:T(8,128)(2,1)} %param.7) | copy-start | bytes 6291460
where the time goes:
time: 54.2 us; the launch traced here: 53.8 us
  blocking collectives  45.9 us (85%)
  matrix products  7.84 us (14%)
    all_gather x1, blocking collectives, shards(): lax.all_gather(row_u, 'row', axis=1, tiled=True)  15.4 us
    all_gather x1, blocking collectives, shards(): lax.all_gather(col_u, 'col', axis=1, tiled=True)  10.9 us
    all_gather x1, blocking collectives, shards(): lax.all_gather(row_v, 'row', axis=1, tiled=True)  9.96 us
    all_gather x1, blocking collectives, shards(): lax.all_gather(col_v, 'col', axis=1, tiled=True)  9.61 us
    dot_general x1, matrix products, shards(): lax.dot_general(lower_flat, upper_flat, (((1,), (1,)), ((), ())), preferr...  2.63 us
    dot_general x1, matrix products, shards(): jnp.einsum('tar,tqr->tqa', right_u, whole_row_v.astype(jnp.float32), prec...  1.79 us
    dot_general x1, matrix products, shards(): jnp.einsum('ba,tbr->tar', diag_upper_inv, whole_col_v.astype(jnp.float32)...  1.77 us

commit v1 on v0

v1 whole, which is shorter than its diff:
```python
import functools

import jax
import jax.numpy as jnp
from jax import lax
from jax.experimental import pallas as pl
from jax.experimental.pallas import tpu as pltpu
from jax.sharding import PartitionSpec as P

MESH = pl.DeviceIdType.MESH
F32 = jnp.float32
BF16 = jnp.bfloat16


def partner(at, step, count):
    if count & (count - 1):
        return lax.rem(at + step, count)
    out = jnp.int32(0)
    weight = 1
    while weight < count:
        bit = (at // weight) % 2
        out = out + weight * ((1 - bit) if step & weight else bit)
        weight *= 2
    return out


def source(at, step, count):
    if count & (count - 1):
        return lax.rem(at + count - step, count)
    return partner(at, step, count)


def split(x):
    high = x.astype(BF16)
    return high, (x - high.astype(F32)).astype(BF16)


def dot(a, b):
    return lax.dot_general(a, b, (((1,), (0,)), ((), ())), preferred_element_type=F32)


def dot_rt(a, b):
    return lax.dot_general(a, b, (((1,), (1,)), ((), ())), preferred_element_type=F32)


def pack(left, right):
    return jnp.concatenate([left.astype(F32), right.astype(F32)], axis=-1).astype(BF16)


def panel_kernel(
    n_row, n_col,
    cu_hbm, cv_hbm, ru_hbm, rv_hbm, dl_hbm, du_hbm, trail_hbm,
    out_ref,
    ru, rv, dl, du, trail, mh, ml, cuall, cvall, gall,
    in_sem, cu_send, cu_recv, cv_send, cv_recv, row_send, row_recv, fwd_send,
):
    row = lax.axis_index("row")
    col = lax.axis_index("col")
    paired = n_row % 2 == 0
    width = 2 if paired else 1
    chips = n_row // width
    core = row % width
    chip = row // width

    col_steps = list(range(n_col - 1, 0, -1))
    chip_steps = list(range(chips - 1, 0, -1))
    col_to = {k: partner(col, k, n_col) for k in col_steps}
    col_from = {k: source(col, k, n_col) for k in col_steps}
    row_to = {k: partner(chip, k, chips) * width + core for k in chip_steps}
    row_from = {k: source(chip, k, chips) * width + core for k in chip_steps}
    mate = chip * width + (1 - core) if paired else row

    barrier = pltpu.get_barrier_semaphore()
    peers = [(row, col_to[k]) for k in col_steps] + [(row_to[k], col) for k in chip_steps]
    if paired:
        peers.append((mate, col))
    for peer in peers:
        pl.semaphore_signal(barrier, inc=1, device_id=peer, device_id_type=MESH)

    loads = []
    for n, (src, dst) in enumerate([
        (ru_hbm, ru), (rv_hbm, rv), (cv_hbm, cvall.at[col]), (cu_hbm, cuall.at[col]),
        (dl_hbm, dl), (du_hbm, du), (trail_hbm, trail),
    ]):
        load = pltpu.make_async_copy(src, dst, in_sem.at[n])
        load.start()
        loads.append(load)

    loads[0].wait()
    loads[1].wait()
    gall[row] = pack(ru[...], rv[...])
    loads[2].wait()
    loads[3].wait()

    pl.semaphore_wait(barrier, len(peers))

    def row_copy(slot, send_sem, to):
        return pltpu.make_async_remote_copy(
            src_ref=gall.at[slot], dst_ref=gall.at[slot], send_sem=send_sem,
            recv_sem=row_recv.at[slot], device_id=(to, col), device_id_type=MESH,
        )

    def col_copy(slots, recv, slot, send_sem, to):
        return pltpu.make_async_remote_copy(
            src_ref=slots.at[slot], dst_ref=slots.at[slot], send_sem=send_sem,
            recv_sem=recv.at[slot], device_id=(row, to), device_id_type=MESH,
        )

    sends = []
    for k in chip_steps:
        sends.append(row_copy(row, row_send.at[k], row_to[k]))
        sends[-1].start()
    for k in col_steps:
        sends.append(col_copy(cvall, cv_recv, col, cv_send.at[k], col_to[k]))
        sends[-1].start()
    for k in col_steps:
        sends.append(col_copy(cuall, cu_recv, col, cu_send.at[k], col_to[k]))
        sends[-1].start()
    if paired:
        sends.append(row_copy(row, row_send.at[0], mate))
        sends[-1].start()

    loads[4].wait()
    loads[5].wait()
    order = dl.shape[0]
    half = order // 2
    uh, ul = split(du[...])
    lh, ll = split(dl[...])

    def product(rows, mid, cols):
        a, b = uh[rows, mid], ul[rows, mid]
        c, d = lh[mid, cols], ll[mid, cols]
        return dot(a, c) + (dot(a, d) + dot(b, c))

    lo, hi, full = slice(0, half), slice(half, order), slice(0, order)
    for rows, mid, cols in ((lo, full, lo), (lo, hi, hi), (hi, hi, lo), (hi, hi, hi)):
        mh[rows, cols], ml[rows, cols] = split(product(rows, mid, cols))

    tiles, rank = cvall.shape[1], cvall.shape[2]
    for k in reversed(col_steps):
        col_copy(cvall, cv_recv, col_from[k], cv_send.at[k], col_to[k]).wait_recv()
    weights = []
    for t in range(tiles):
        turned = jnp.concatenate([cvall[c, t] for c in range(n_col)], axis=-1)
        wh, wl = split(dot(turned, mh[...]) + dot(turned, ml[...]))
        weights.append(jnp.concatenate([wh, wl], axis=0))

    for k in reversed(col_steps):
        col_copy(cuall, cu_recv, col_from[k], cu_send.at[k], col_to[k]).wait_recv()
    lefts = []
    for t in range(tiles):
        turned = jnp.concatenate([cuall[c, t] for c in range(n_col)], axis=-1).astype(F32)
        lefts.append(jnp.concatenate([turned, turned], axis=0).T.astype(BF16))

    for k in reversed(chip_steps):
        slot = row_from[k]
        row_copy(slot, row_send.at[k], row_to[k]).wait_recv()
        if paired:
            sends.append(row_copy(slot, fwd_send.at[k], mate))
            sends[-1].start()
    if paired:
        row_copy(mate, row_send.at[0], mate).wait_recv()
        for k in reversed(chip_steps):
            slot = source(chip, k, chips) * width + (1 - core)
            row_copy(slot, fwd_send.at[k], mate).wait_recv()
    loads[6].wait()

    for j in range(gall.shape[1]):
        g = gall[:, j].reshape(order, 2 * rank)
        at = pl.ds(j * order, order)
        for t in range(tiles):
            c = dot(weights[t], g)
            c = c[:rank, :rank] + c[rank:, :rank]
            ch, cl = split(jnp.concatenate([jnp.zeros_like(c), c], axis=-1))
            right = dot_rt(jnp.concatenate([ch, cl], axis=0), g)
            th, tl = split(right[:rank] + right[rank:])
            update = dot(lefts[t], jnp.concatenate([th, tl], axis=0))
            rows = pl.ds(t * order, order)
            out_ref[rows, at] = (trail[rows, at].astype(F32) - update).astype(BF16)

    for send in sends:
        send.wait_send()


def shards(n_row, n_col, trailing, col_u, col_v, row_u, row_v, diag_lower_inv, diag_upper_inv):
    mt, cc, rank = col_u.shape
    nt, rc, _ = row_u.shape
    order = diag_lower_inv.shape[0]
    anywhere = pl.BlockSpec(memory_space=pl.ANY)
    dma = pltpu.SemaphoreType.DMA
    return pl.pallas_call(
        functools.partial(panel_kernel, n_row, n_col),
        out_shape=pltpu.VMEM(trailing.shape, BF16),
        in_specs=[anywhere] * 7,
        out_specs=pl.BlockSpec(memory_space=pltpu.VMEM),
        scratch_shapes=[
            pltpu.VMEM(row_u.shape, BF16),
            pltpu.VMEM(row_v.shape, BF16),
            pltpu.VMEM((order, order), F32),
            pltpu.VMEM((order, order), F32),
            pltpu.VMEM(trailing.shape, BF16),
            pltpu.VMEM((order, order), BF16),
            pltpu.VMEM((order, order), BF16),
            pltpu.VMEM((n_col, mt, rank, cc), BF16),
            pltpu.VMEM((n_col, mt, rank, cc), BF16),
            pltpu.VMEM((n_row, nt, rc, 2 * rank), BF16),
            dma((7,)), dma((n_col,)), dma((n_col,)), dma((n_col,)), dma((n_col,)),
            dma((n_row,)), dma((n_row,)), dma((n_row,)),
        ],
        compiler_params=pltpu.CompilerParams(collective_id=0, has_side_effects=True),
        name="panels",
    )(
        jnp.swapaxes(col_u, 1, 2), jnp.swapaxes(col_v, 1, 2), row_u, row_v,
        diag_lower_inv, diag_upper_inv, trailing,
    )


def solution(mesh):
    placed = (
        P("row", "col"),
        P("row", "col", None),
        P("row", "col", None),
        P("col", "row", None),
        P("col", "row", None),
        P(),
        P(),
    )
    return jax.shard_map(
        functools.partial(shards, mesh.shape["row"], mesh.shape["col"]),
        mesh=mesh, in_specs=placed, out_specs=P("row", "col"), check_vma=False,
    )
```

time: 54.2 us -> 15.3 us (0.28)
  blocking collectives: 45.9 us -> 0 us
  Pallas kernels: 0 us -> 13.8 us
  matrix products: 7.84 us -> 0 us
  local copies, waits for them, and re-layouts: 0.02 us -> 1.32 us
    all_gather x4 -> x0, blocking collectives: 45.9 us -> none  [the longest x1 15.4 us: shards(): lax.all_gather(row_u, 'row', axis=1, tiled=True)]
    pallas_call x0 -> x1, Pallas kernels: none -> 13.8 us  [shards(): pl.pallas_call(functools.partial(panel_kernel, n_row, n_col), out_shape=p...]
    dot_general x5 -> x0, matrix products: 7.84 us -> none  [the longest x1 2.63 us: shards(): lax.dot_general(lower_flat, upper_flat, (((1,), (1,)), ((), ())), preferr...]
    unnamed x8 -> x1, local copies, waits for them, and re-layouts: 0.02 us -> 1.32 us
where the time goes in v1:
time: 15.3 us; the launch traced here: 15.1 us
  Pallas kernels  13.8 us (90%)
  local copies, waits for them, and re-layouts  1.32 us (9%)
    pallas_call x1, Pallas kernels, shards(): pl.pallas_call(functools.partial(panel_kernel, n_row, n_col), out_shape=p...  13.8 us
    unnamed x1, local copies, waits for them, and re-layouts  1.32 us

profile of v1, /device:TPU:1, one launch (start us, length us, event | category | flops | bytes accessed | tf_op | source)
XLA Modules:
  0.0 15.1 jit_solution(5003691537063740416)
XLA Ops:
  0.0 13.8 %panels.1 = bf16[512,2048]{1,0:T(8,128)(2,1)S(1)} custom-call(bf16[1,64,128]{2,1,0:T(8,128)(2,1)} %bitcast.2, bf16[1,64,128]{2,1,0:T(8,128)(2,1)} %bitcast.3, bf16[4,64,64]{2,1,0:T(8,128)(2,1)} %ru_hbm.1, bf16[4,64,64]{2,1,0:T(8,128)(2,1)} %rv_hbm.1, f32[512,512]{1,0:T(8,128)} %dl_hbm.1, f32[512,512]{1,0:T(8,128)} %du_hbm.1, bf16[512,2048]{1,0:T(8,128)(2,1)} %trail_hbm.1), custom_call_target="tpu_custom_call" | custom-call | tf_op jit(solution)/shard_map/panels/pallas_call | solution.py:191
  13.8 1.3 %copy.9 = bf16[512,2048]{1,0:T(8,128)(2,1)} copy(bf16[512,2048]{1,0:T(8,128)(2,1)S(1)} %panels.1) | data formatting | bytes 4194304

commit v2 on v1

--- a/solution.py
+++ b/solution.py
@@ -10,6 +10,7 @@
 MESH = pl.DeviceIdType.MESH
 F32 = jnp.float32
 BF16 = jnp.bfloat16
+BLOCKS = 1
 
 
 def partner(at, step, count):
@@ -50,8 +51,8 @@
 def panel_kernel(
     n_row, n_col,
     cu_hbm, cv_hbm, ru_hbm, rv_hbm, dl_hbm, du_hbm, trail_hbm,
-    out_ref,
-    ru, rv, dl, du, trail, mh, ml, cuall, cvall, gall,
+    t_ref, cu_ref, trail,
+    ru, rv, dl, du, mh, ml, cuall, cvall, gall,
     in_sem, cu_send, cu_recv, cv_send, cv_recv, row_send, row_recv, fwd_send,
 ):
     row = lax.axis_index("row")
@@ -136,28 +137,29 @@
     for rows, mid, cols in ((lo, full, lo), (lo, hi, hi), (hi, hi, lo), (hi, hi, hi)):
         mh[rows, cols], ml[rows, cols] = split(product(rows, mid, cols))
 
-    tiles, rank = cvall.shape[1], cvall.shape[2]
-    for k in reversed(col_steps):
-        col_copy(cvall, cv_recv, col_from[k], cv_send.at[k], col_to[k]).wait_recv()
-    weights = []
-    for t in range(tiles):
-        turned = jnp.concatenate([cvall[c, t] for c in range(n_col)], axis=-1)
-        wh, wl = split(dot(turned, mh[...]) + dot(turned, ml[...]))
-        weights.append(jnp.concatenate([wh, wl], axis=0))
-
-    for k in reversed(col_steps):
-        col_copy(cuall, cu_recv, col_from[k], cu_send.at[k], col_to[k]).wait_recv()
-    lefts = []
-    for t in range(tiles):
-        turned = jnp.concatenate([cuall[c, t] for c in range(n_col)], axis=-1).astype(F32)
-        lefts.append(jnp.concatenate([turned, turned], axis=0).T.astype(BF16))
-
     for k in reversed(chip_steps):
         slot = row_from[k]
         row_copy(slot, row_send.at[k], row_to[k]).wait_recv()
         if paired:
             sends.append(row_copy(slot, fwd_send.at[k], mate))
             sends[-1].start()
+
+    tiles, rank = cvall.shape[1], cvall.shape[2]
+    for k in reversed(col_steps):
+        col_copy(cvall, cv_recv, col_from[k], cv_send.at[k], col_to[k]).wait_recv()
+    weights = []
+    for t in range(tiles):
+        turned = jnp.concatenate([cvall[c, t] for c in range(n_col)], axis=-1)
+        wh, wl = split(dot(turned, mh[...]) + dot(turned, ml[...]))
+        weights.append(jnp.concatenate([wh, wl], axis=0))
+
+    for k in reversed(col_steps):
+        col_copy(cuall, cu_recv, col_from[k], cu_send.at[k], col_to[k]).wait_recv()
+    lefts = []
+    for t in range(tiles):
+        turned = jnp.concatenate([cuall[c, t] for c in range(n_col)], axis=-1).astype(F32)
+        lefts.append(jnp.concatenate([turned, turned], axis=0).T.astype(BF16))
+
     if paired:
         row_copy(mate, row_send.at[0], mate).wait_recv()
         for k in reversed(chip_steps):
@@ -165,21 +167,41 @@
             row_copy(slot, fwd_send.at[k], mate).wait_recv()
     loads[6].wait()
 
-    for j in range(gall.shape[1]):
-        g = gall[:, j].reshape(order, 2 * rank)
-        at = pl.ds(j * order, order)
-        for t in range(tiles):
-            c = dot(weights[t], g)
-            c = c[:rank, :rank] + c[rank:, :rank]
-            ch, cl = split(jnp.concatenate([jnp.zeros_like(c), c], axis=-1))
+    panels = [gall[:, j].reshape(order, 2 * rank) for j in range(gall.shape[1])]
+    spread = jnp.concatenate(panels, axis=-1)
+    for t in range(tiles):
+        c = dot(weights[t], spread)
+        c = c[:rank] + c[rank:]
+        rights = []
+        for j, g in enumerate(panels):
+            core_j = c[:, 2 * rank * j:2 * rank * j + rank]
+            ch, cl = split(jnp.concatenate([jnp.zeros_like(core_j), core_j], axis=-1))
             right = dot_rt(jnp.concatenate([ch, cl], axis=0), g)
             th, tl = split(right[:rank] + right[rank:])
-            update = dot(lefts[t], jnp.concatenate([th, tl], axis=0))
-            rows = pl.ds(t * order, order)
-            out_ref[rows, at] = (trail[rows, at].astype(F32) - update).astype(BF16)
+            rights.append(jnp.concatenate([th, tl], axis=0))
+        cu_ref[t] = lefts[t]
+        for j, right in enumerate(rights):
+            t_ref[t, :, pl.ds(j * order, order)] = right
 
     for send in sends:
         send.wait_send()
+
+
+def update_kernel(blocks, t_ref, cu_ref, trail, out_hbm, out, out_sem):
+    tiles, order, _ = cu_ref.shape
+    wide = t_ref.shape[2] // blocks
+    copies = []
+    for t in range(tiles):
+        rows = pl.ds(t * order, order)
+        for b in range(blocks):
+            at = pl.ds(b * wide, wide)
+            product = dot(cu_ref[t], t_ref[t, :, at])
+            out[rows, at] = (trail[rows, at].astype(F32) - product).astype(BF16)
+            copy = pltpu.make_async_copy(out.at[rows, at], out_hbm.at[rows, at], out_sem.at[t * blocks + b])
+            copy.start()
+            copies.append(copy)
+    for copy in copies:
+        copy.wait()
 
 
 def shards(n_row, n_col, trailing, col_u, col_v, row_u, row_v, diag_lower_inv, diag_upper_inv):
@@ -188,17 +210,22 @@
     order = diag_lower_inv.shape[0]
     anywhere = pl.BlockSpec(memory_space=pl.ANY)
     dma = pltpu.SemaphoreType.DMA
-    return pl.pallas_call(
+    wide = nt * order
+    vmem = pl.BlockSpec(memory_space=pltpu.VMEM)
+    handed = pl.pallas_call(
         functools.partial(panel_kernel, n_row, n_col),
-        out_shape=pltpu.VMEM(trailing.shape, BF16),
+        out_shape=[
+            pltpu.VMEM((mt, 2 * rank, wide), BF16),
+            pltpu.VMEM((mt, order, 2 * rank), BF16),
+            pltpu.VMEM(trailing.shape, BF16),
+        ],
         in_specs=[anywhere] * 7,
-        out_specs=pl.BlockSpec(memory_space=pltpu.VMEM),
+        out_specs=[vmem] * 3,
         scratch_shapes=[
             pltpu.VMEM(row_u.shape, BF16),
             pltpu.VMEM(row_v.shape, BF16),
             pltpu.VMEM((order, order), F32),
             pltpu.VMEM((order, order), F32),
-            pltpu.VMEM(trailing.shape, BF16),
             pltpu.VMEM((order, order), BF16),
             pltpu.VMEM((order, order), BF16),
             pltpu.VMEM((n_col, mt, rank, cc), BF16),
@@ -213,6 +240,16 @@
         jnp.swapaxes(col_u, 1, 2), jnp.swapaxes(col_v, 1, 2), row_u, row_v,
         diag_lower_inv, diag_upper_inv, trailing,
     )
+    handed = [pltpu.with_memory_space_constraint(x, pltpu.VMEM) for x in handed]
+    blocks = BLOCKS * nt
+    return pl.pallas_call(
+        functools.partial(update_kernel, blocks),
+        out_shape=jax.ShapeDtypeStruct(trailing.shape, BF16),
+        in_specs=[vmem] * 3,
+        out_specs=anywhere,
+        scratch_shapes=[pltpu.VMEM(trailing.shape, BF16), dma((mt * blocks,))],
+        name="update",
+    )(*handed)
 
 
 def solution(mesh):

time: 15.3 us -> 13.6 us (0.89)
  local copies, waits for them, and re-layouts: 1.32 us -> 0 us
  Pallas kernels: 13.8 us -> 13.4 us
    unnamed x1 -> x0, local copies, waits for them, and re-layouts: 1.32 us -> none
    pallas_call x1 -> x2, Pallas kernels: 13.8 us -> 13.4 us  [the longest x1 11.8 us: shards(): pl.pallas_call(functools.partial(panel_kernel, n_row, n_col), out_shape=[...]
where the time goes in v2:
time: 13.6 us; the launch traced here: 13.5 us
  Pallas kernels  13.4 us (99%)
    pallas_call x1, Pallas kernels, shards(): pl.pallas_call(functools.partial(panel_kernel, n_row, n_col), out_shape=[...  11.8 us
    pallas_call x1, Pallas kernels, shards(): pl.pallas_call(functools.partial(update_kernel, blocks), out_shape=jax.Sh...  1.63 us

profile of v2, /device:TPU:1, one launch (start us, length us, event | category | flops | bytes accessed | tf_op | source)
XLA Modules:
  0.0 13.5 jit_solution(7967120743054139172)
XLA Ops:
  0.0 11.8 %panels.1 = (bf16[1,128,2048]{2,1,0:T(8,128)(2,1)S(1)}, bf16[1,512,128]{2,1,0:T(8,128)(2,1)S(1)}, bf16[512,2048]{1,0:T(8,128)(2,1)S(1)}) custom-call(bf16[1,64,128]{2,1,0:T(8,128)(2,1)} %bitcast.2, bf16[1,64,128]{2,1,0:T(8,128)(2,1)} %bitcast.3, bf16[4,64,64]{2,1,0:T(8,128)(2,1)} %ru_hbm.1, bf16[4,64,64]{2,1,0:T(8,128)(2,1)} %rv_hbm.1, f32[512,512]{1,0:T(8,128)} %dl_hbm.1, ...), custom_call_target="tpu_custom_call" | custom-call | tf_op jit(solution)/shard_map/panels/pallas_call | solution.py:215
  11.8 1.6 %update.1 = bf16[512,2048]{1,0:T(8,128)(2,1)} custom-call(bf16[1,128,2048]{2,1,0:T(8,128)(2,1)S(1)} %get-tuple-element.8.t_ref, bf16[1,512,128]{2,1,0:T(8,128)(2,1)S(1)} %get-tuple-element.9.cu_ref, bf16[512,2048]{1,0:T(8,128)(2,1)S(1)} %get-tuple-element.10.trail), custom_call_target="tpu_custom_call" | custom-call | tf_op jit(solution)/shard_map/update/pallas_call | solution.py:245
